TPU v7x, 32 devices: a 4x4x1 block of a 4x4x8 slice. The times are simulated.
32 devices in a mesh: dp: 2 (over z, core), ep: 16 (over x, y).
Axes of the slice: x: 4, y: 4, z: 1, core: 2. Of those that a mesh axis runs over, the one named last changes fastest.
The devices are a block of a 4x4x8 slice.
Arguments:
- x: bfloat16 [2, 16, 256, 1792], P('dp', 'ep'), parts along dimension 0
- expert: int32 [2, 16, 256, 2], P('dp', 'ep'), parts along dimension 0
- slot: int32 [2, 16, 256, 2], P('dp', 'ep'), parts along dimension 0
- gate: float32 [2, 16, 256, 2], P('dp', 'ep'), parts along dimension 0
- w_gate: bfloat16 [32, 1792, 4864], P('ep')
- w_up: bfloat16 [32, 1792, 4864], P('ep')
- w_down: bfloat16 [32, 4864, 1792], P('ep')
Outputs:
- y: bfloat16 [2, 16, 256, 1792], P('dp', 'ep'), parts along dimension 0
There are 2 independent parts. A program takes and returns all parts, laid end to end along the dimension named above; an argument that names none is the same for every part.
All inputs are finite; a program needn't handle non-finite values.
Results may differ from a plain program's by a relative error of at most 0.009.
Values are sent between devices in bfloat16 or wider.
A program may use at most 768 MiB of HBM per device.

v0:
```python
import jax
import jax.numpy as jnp
from jax import lax
from jax.sharding import NamedSharding, PartitionSpec as P


def einsum(form, a, b):
    return jnp.einsum(form, a.astype(jnp.float32), b.astype(jnp.float32))


def solution(mesh):
    def placed(v, *spec):
        return lax.with_sharding_constraint(v, NamedSharding(mesh, P(*spec)))

    def step(x, expert, slot, gate, w_gate, w_up, w_down):
        experts, (tokens, top) = w_gate.shape[0], expert.shape[2:]
        slots = 5 * tokens * top // (4 * experts)
        to_expert = jax.nn.one_hot(expert, experts, dtype=jnp.bfloat16)
        to_slot = jax.nn.one_hot(slot, slots, dtype=jnp.bfloat16)
        weighted = to_expert * gate[..., None].astype(jnp.bfloat16)
        dispatch = einsum("abtke,abtkc->abtec", to_expert, to_slot).astype(jnp.bfloat16)
        combine = einsum("abtke,abtkc->abtec", weighted, to_slot).astype(jnp.bfloat16)
        z = einsum("abtec,abtd->aebcd", dispatch, x).astype(jnp.bfloat16)
        z = placed(z, "dp", None, "ep", None, None)
        z = placed(z, "dp", "ep", None, None, None)
        h = jax.nn.silu(einsum("aebcd,edf->aebcf", z, w_gate))
        h = (h * einsum("aebcd,edf->aebcf", z, w_up)).astype(jnp.bfloat16)
        out = einsum("aebcf,efd->aebcd", h, w_down).astype(jnp.bfloat16)
        out = placed(out, "dp", "ep", None, None, None)
        out = placed(out, "dp", None, "ep", None, None)
        y = einsum("abtec,aebcd->abtd", combine, out)
        return y.astype(jnp.bfloat16)

    return step
```

profile of v0, /device:TPU:96, one launch (start us, length us, event | category | flops | bytes accessed | tf_op | source)
XLA Modules:
  0.0 180.5 jit_solution(474599284164304063)
XLA Ops:
  0.0 0.0 copy-start
  0.0 0.9 copy.11
  0.9 0.0 copy-start.2
  0.9 0.8 copy.9
  1.8 0.7 copy-done.4
  2.4 2.8 %convolution_convert_fusion.1 = bf16[256,32,20]{1,2,0:T(8,128)(2,1)S(1)} fusion(s32[256,2]{1,0:T(8,128)S(1)} %copy.11, s32[256,2]{1,0:T(8,128)S(1)} %copy.9), kind=kOutput, calls=%fused_computation.25 | convolution fusion | flops 845824 | bytes 331776 | tf_op jit(solution)/abtke,abtkc->abtec/dot_general | solution.py:8
  5.2 0.0 copy-done
  5.2 1.1 convolution_convert_fusion
  6.3 2.3 %reshape.6 = bf16[1,16,2,1,20,1792]{5,2,1,4,3,0:T(2,128)(2,1)} reshape(bf16[32,20,1792]{2,0,1:T(8,128)(2,1)S(1)} %convolution_convert_fusion) | data formatting | bytes 4587520 | tf_op jit(solution)/sharding_constraint;jit(solution)/sharding_constraint | solution.py:13
  8.6 3.2 %copy.13 = bf16[1,16,2,1,20,1792]{5,2,4,3,0,1:T(2,128)(2,1)S(1)} copy(bf16[1,16,2,1,20,1792]{5,2,1,4,3,0:T(2,128)(2,1)} %reshape.6) | data formatting | bytes 4587520 | tf_op jit(solution)/sharding_constraint;jit(solution)/sharding_constraint | solution.py:13
  11.9 40.5 %all-to-all.4 = bf16[1,16,2,1,20,1792]{5,2,4,3,0,1:T(2,128)(2,1)S(1)} all-to-all(bf16[1,16,2,1,20,1792]{5,2,4,3,0,1:T(2,128)(2,1)S(1)} %copy.13), channel_id=1, replica_groups=mesh['dp'=2,'ep'=16] {'ep'}, dimensions={1} | all-to-all | bytes 4587520 | tf_op jit(solution)/sharding_constraint;jit(solution)/sharding_constraint | solution.py:13
  52.4 23.1 %fusion.4 = f32[2,16,20,4864]{3,2,1,0:T(8,128)} fusion(bf16[2,1792,4864]{2,1,0:T(8,128)(2,1)} %param.4, bf16[1,16,2,1,20,1792]{5,2,4,3,0,1:T(2,128)(2,1)S(1)} %all-to-all.4), kind=kOutput, calls=%fused_computation.4 | convolution fusion | flops 11156848640 | bytes 49610752 | tf_op jit(solution)/aebcd,edf->aebcf/dot_general | solution.py:8
  75.5 27.6 %fusion.12.clone.8 = bf16[2,16,20,4864]{3,2,1,0:T(8,128)(2,1)} fusion(bf16[2,1792,4864]{2,1,0:T(8,128)(2,1)} %param.5, f32[2,16,20,4864]{3,2,1,0:T(8,128)} %fusion.4, bf16[1,16,2,1,20,1792]{5,2,4,3,0,1:T(2,128)(2,1)S(1)} %all-to-all.4), kind=kOutput, calls=%fused_computation.13.clone.clone.clone.clone.clone.clone.clone.1 | convolution fusion | flops 11175526400 | bytes 55836672 | tf_op jit(solution)/aebcd,edf->aebcf/dot_general | solution.py:8
  103.0 22.1 %fusion.23 = bf16[1,2,16,1,20,1792]{5,4,2,1,3,0:T(8,128)(2,1)} fusion(bf16[2,4864,1792]{2,1,0:T(8,128)(2,1)} %param.6, bf16[2,16,20,4864]{3,2,1,0:T(8,128)(2,1)} %fusion.12.clone.8), kind=kOutput, calls=%fused_computation.17 | convolution fusion | flops 11157995520 | bytes 43384832 | tf_op jit(solution)/aebcf,efd->aebcd/dot_general | solution.py:8
  125.1 5.6 %copy.15 = bf16[1,2,16,1,20,1792]{5,1,4,3,0,2:T(2,128)(2,1)} copy(bf16[1,2,16,1,20,1792]{5,4,2,1,3,0:T(8,128)(2,1)} %fusion.23) | data formatting | bytes 4587520 | tf_op jit(solution)/sharding_constraint;jit(solution)/sharding_constraint | solution.py:13
  130.7 4.6 %all-to-all-start.1 = ((bf16[1,2,16,1,20,1792]{5,1,4,3,0,2:T(2,128)(2,1)}), bf16[1,2,16,1,20,1792]{5,1,4,3,0,2:T(2,128)(2,1)S(1)}, u32[]{:S(2)}, u32[]{:S(2)}) async-start(bf16[1,2,16,1,20,1792]{5,1,4,3,0,2:T(2,128)(2,1)} %copy.15), calls=%async_computation.1 | async-start | bytes 4587520 | tf_op jit(solution)/sharding_constraint;jit(solution)/sharding_constraint | solution.py:13
  135.3 0.1 copy.10
  135.4 0.0 copy-done.3
  135.4 3.9 %convolution_convert_fusion.2 = bf16[256,32,20]{1,2,0:T(8,128)(2,1)} fusion(s32[256,2]{1,0:T(8,128)S(1)} %copy-done.3, s32[256,2]{1,0:T(8,128)S(1)} %copy-done.5, bf16[256,2]{1,0:T(8,128)(2,1)S(1)} %copy.10), kind=kOutput, calls=%fused_computation.26 | convolution fusion | flops 862208 | bytes 332800 | tf_op jit(solution)/abtke,abtkc->abtec/dot_general | solution.py:8
  139.3 29.0 %all-to-all-done.1 = bf16[1,2,16,1,20,1792]{5,1,4,3,0,2:T(2,128)(2,1)S(1)} async-done(((bf16[1,2,16,1,20,1792]{5,1,4,3,0,2:T(2,128)(2,1)}), bf16[1,2,16,1,20,1792]{5,1,4,3,0,2:T(2,128)(2,1)S(1)}, u32[]{:S(2)}, u32[]{:S(2)}) %all-to-all-start.1) | async-done | bytes 2293792 | tf_op jit(solution)/sharding_constraint;jit(solution)/sharding_constraint | solution.py:13
  168.3 3.7 %copy.16 = bf16[1,16,2,1,20,1792]{5,2,1,4,3,0:T(2,128)(2,1)} copy(bf16[1,16,2,1,20,1792]{5,2,4,3,0,1:T(2,128)(2,1)S(1)} %bitcast.132) | data formatting | bytes 4587520 | tf_op jit(solution)/sharding_constraint;jit(solution)/sharding_constraint | solution.py:13
  172.0 4.8 %reshape.46 = bf16[32,20,1792]{2,0,1:T(8,128)(2,1)S(1)} reshape(bf16[1,16,2,1,20,1792]{5,2,1,4,3,0:T(2,128)(2,1)} %copy.16) | data formatting | bytes 4587520
  176.9 0.0 copy-start.1
  176.9 3.6 %fusion.35 = bf16[1,1,256,1792]{3,2,1,0:T(8,128)(2,1)} fusion(bf16[32,20,1792]{2,0,1:T(8,128)(2,1)S(1)} %reshape.46, bf16[256,32,20]{1,2,0:T(8,128)(2,1)} %convolution_convert_fusion.2), kind=kOutput, calls=%fused_computation.24 | convolution fusion | flops 587661312 | bytes 3538944 | tf_op jit(solution)/abtec,aebcd->abtd/dot_general | solution.py:8
  (9 shorter events, 0.0 us)
Async XLA Ops:
  0.0 5.2 %copy-start = (bf16[1,1,256,1792]{3,2,1,0:T(8,128)(2,1)S(1)}, bf16[1,1,256,1792]{3,2,1,0:T(8,128)(2,1)}, u32[]{:S(2)}) copy-start(bf16[1,1,256,1792]{3,2,1,0:T(8,128)(2,1)} %param.3) | copy-start | bytes 2752516
  0.9 0.9 copy-start.2
  1.8 0.7 copy-start.4
  130.7 4.6 %copy-start.6 = (f32[1,1,256,2]{2,3,1,0:T(2,128)S(1)}, f32[1,1,256,2]{2,3,1,0:T(2,128)}, u32[]{:S(2)}) copy-start(f32[1,1,256,2]{2,3,1,0:T(2,128)} %param.1) | copy-start | bytes 6148
  130.7 4.7 %copy-start.3 = (s32[256,2]{1,0:T(8,128)S(1)}, s32[256,2]{1,0:T(8,128)}, u32[]{:S(2)}) copy-start(s32[256,2]{1,0:T(8,128)} %copy-done.2) | copy-start | bytes 6148
  130.7 4.7 %copy-start.5 = (s32[256,2]{1,0:T(8,128)S(1)}, s32[256,2]{1,0:T(8,128)}, u32[]{:S(2)}) copy-start(s32[256,2]{1,0:T(8,128)} %copy-done.4) | copy-start | bytes 6148
  130.7 37.6 %all-to-all-start.1 = ((bf16[1,2,16,1,20,1792]{5,1,4,3,0,2:T(2,128)(2,1)}), bf16[1,2,16,1,20,1792]{5,1,4,3,0,2:T(2,128)(2,1)S(1)}, u32[]{:S(2)}, u32[]{:S(2)}) async-start(bf16[1,2,16,1,20,1792]{5,1,4,3,0,2:T(2,128)(2,1)} %copy.15), calls=%async_computation.1 | async-start | bytes 4587520 | tf_op jit(solution)/sharding_constraint;jit(solution)/sharding_constraint | solution.py:13
  176.9 3.7 %copy-start.1 = (bf16[1,1,256,1792]{3,2,1,0:T(8,128)(2,1)S(1)}, bf16[1,1,256,1792]{3,2,1,0:T(8,128)(2,1)}, u32[]{:S(2)}) copy-start(bf16[1,1,256,1792]{3,2,1,0:T(8,128)(2,1)} %param.3) | copy-start | bytes 2752516
where the time goes:
time: 181 us
  matrix products  84.1 us (46%)
  blocking collectives  40.5 us (22%)
  waiting for transfers between devices  29 us (16%)
  local copies, waits for them, and re-layouts  22.2 us (12%)
  starting transfers between devices  4.56 us (3%)
    dot_general x7, matrix products, einsum(): return jnp.einsum(form, a.astype(jnp.float32), b.astype(jnp.float32))  84.1 us
    another operation x1, blocking collectives, placed(): return lax.with_sharding_constraint(v, NamedSharding(mesh, P(*spec)))  40.5 us
    another operation x1, waiting for transfers between devices, placed(): return lax.with_sharding_constraint(v, NamedSharding(mesh, P(*spec)))  29 us
    another operation x4, local copies, waits for them, and re-layouts, placed(): return lax.with_sharding_constraint(v, NamedSharding(mesh, P(*spec)))  14.8 us
    unnamed x17, local copies, waits for them, and re-layouts  7.26 us
    another operation x1, starting transfers between devices, placed(): return lax.with_sharding_constraint(v, NamedSharding(mesh, P(*spec)))  4.56 us
  transfers between devices with their start and end apart: 1, of which 1 were waited for; matrix products, arithmetic and copies ran while one was open for 2% of the time, Pallas kernels for 0%

commit v1 on v0

v1 whole, which is shorter than its diff:
```python
import functools

import jax
import jax.numpy as jnp
from jax import lax
from jax.experimental import pallas as pl
from jax.experimental.pallas import tpu as pltpu
from jax.sharding import PartitionSpec as P

MESH = pl.DeviceIdType.MESH
FT = 256
NT = 512
ROWS = 16
UNROLL = 3


def dot(a, b):
    return jnp.dot(a, b, preferred_element_type=jnp.float32)


def kernel(
    side, slots,
    x_hbm, expert_ref, slot_ref, gate_ref, wg, wu, wd, y_hbm,
    xs, gu, dn, h, zc, snd, snd_c, rcv, rcv_c, ret, ret_c,
    sem_x, sem_g, sem_d, sem_ds, sem_dr, sem_cs, sem_cr, sem_y,
):
    members = side * side
    tokens, width = xs.shape
    hidden = h.shape[1]
    steps = hidden // FT
    rest = slots - ROWS
    dp, ep = lax.axis_index("dp"), lax.axis_index("ep")
    core = lax.rem(dp, 2)
    base = dp - core
    px, py = ep // side, lax.rem(ep, side)
    tiles = [(n, min(NT, width - n)) for n in range(0, width, NT)]
    blocks = members

    def place(i, chunk):
        dx = i // (2 * side)
        return (dx if chunk == 2 else 2 * dx + chunk), (i // 2) % side

    def ahead(i, chunk):
        dx, dy = place(i, chunk)
        return ((px + dx) % side) * side + (py + dy) % side

    def behind(i, chunk):
        dx, dy = place(i, chunk)
        return ((px + side - dx) % side) * side + (py + side - dy) % side

    def others(chunk):
        return {0: blocks - 1, 1: blocks, 2: 2 * blocks - 1}[chunk]

    def block_of(i, chunk):
        if chunk == 1:
            return i
        i = i + 1
        return i // 2 * 2 + (i + core) % 2

    copy_x = pltpu.make_async_copy(x_hbm.at[0, 0], xs, sem_x)
    copy_x.start()

    barrier = pltpu.get_barrier_semaphore()

    def greet(i, c):
        j = block_of(i, 2)
        pl.semaphore_signal(
            barrier, inc=1, device_id=(base + j % 2, ahead(j, 2)), device_id_type=MESH
        )
        return c

    lax.fori_loop(0, others(2), greet, 0)

    def gu_copies(s):
        cols = pl.ds(pl.multiple_of(s * FT, FT), FT)
        return (
            pltpu.make_async_copy(wg.at[core, :, cols], gu.at[s, :, pl.ds(0, FT)], sem_g.at[s, 0]),
            pltpu.make_async_copy(wu.at[core, :, cols], gu.at[s, :, pl.ds(FT, FT)], sem_g.at[s, 1]),
        )

    def dn_copy(t):
        n, size = tiles[t]
        return pltpu.make_async_copy(wd.at[core, :, pl.ds(n, size)], dn.at[:, pl.ds(n, size)], sem_d.at[t])

    copy_x.wait()

    def start_gu(s, c):
        for copy in gu_copies(s):
            copy.start()
        return c

    lax.fori_loop(0, steps, start_gu, 0)
    for t in range(len(tiles)):
        dn_copy(t).start()

    slot, expert = slot_ref[0, 0], expert_ref[0, 0]
    code = jnp.where(slot < slots, expert * slots + slot, -1)
    down0, down1 = code[:, 0:1], code[:, 1:2]
    across0 = jnp.transpose(jnp.broadcast_to(down0, (tokens, 128)))[0:1]
    across1 = jnp.transpose(jnp.broadcast_to(down1, (tokens, 128)))[0:1]
    gates = gate_ref[0, 0].astype(jnp.bfloat16).astype(jnp.float32)

    def row_code(row, chunk):
        i, j = row // 16, row % 16
        if chunk == 2:
            return (2 * ahead(i, 2) + i % 2) * slots + ROWS + j % 4, j // 4
        return (2 * ahead(i, chunk) + i % 2) * slots + j, None

    def gather_mask(chunk, rows):
        row = lax.broadcasted_iota(jnp.int32, (rows, tokens), 0)
        code, quarter = row_code(row, chunk)
        hit = (code == across0) | (code == across1)
        if chunk == 2:
            hit = hit & (row % 4 < rest)
        return hit, quarter

    def ones(mask):
        return jnp.where(mask, 1.0, 0.0).astype(jnp.bfloat16)

    def send(chunk, src, dst, n, size, s_sem, r_sem, target):
        def one(i, c):
            j = block_of(i, chunk)
            there = j // 2 * 2 + core
            cols = pl.ds(n, size)
            pltpu.make_async_remote_copy(
                src_ref=src.at[j, :, cols],
                dst_ref=dst.at[there, :, cols],
                send_sem=s_sem,
                recv_sem=r_sem,
                device_id=(base + j % 2, target(j, chunk)),
                device_id_type=MESH,
            ).start()
            return c

        lax.fori_loop(0, others(chunk), one, 0)

    def wait(chunk, ref, n, size, sem):
        part = ref.at[pl.ds(0, others(chunk)), :, pl.ds(n, size)]
        pltpu.make_async_copy(part, part, sem).wait()

    rows_c = 2 * blocks * 16
    hit, quarter = gather_mask(2, rows_c)
    picks = [ones(hit & (quarter == q)) for q in range(4)]
    for n in range(0, NT, FT):
        total = None
        for q in range(4):
            if q * NT + n < width:
                part = dot(picks[q], xs[:, q * NT + n : q * NT + n + FT])
                total = part if total is None else total + part
        snd_c[:, :, n : n + FT] = total.astype(jnp.bfloat16).reshape(2 * blocks, 16, FT)
    rcv_c[core] = snd_c[core]

    pl.semaphore_wait(barrier, others(2))
    send(2, snd_c, rcv_c, 0, NT, sem_ds.at[2], sem_dr.at[2], ahead)
    for chunk in range(2):
        hit, _ = gather_mask(chunk, blocks * 16)
        pick = ones(hit)
        for n, size in tiles:
            z = dot(pick, xs[:, n : n + size]).astype(jnp.bfloat16)
            snd[chunk, :, :, n : n + size] = z.reshape(blocks, 16, size)
        if chunk == 0:
            rcv[0, core] = snd[0, core]
        send(chunk, snd.at[chunk], rcv.at[chunk], 0, width, sem_ds.at[chunk], sem_dr.at[chunk], ahead)

    rows_z = zc.shape[0]

    def unstack(q):
        r = lax.broadcasted_iota(jnp.int32, (rows_z, rows_c), 0)
        s = lax.broadcasted_iota(jnp.int32, (rows_z, rows_c), 1)
        return ones(s == (r // 4) * 16 + q * 4 + r % 4)

    def stack(q):
        s = lax.broadcasted_iota(jnp.int32, (rows_c, rows_z), 0)
        r = lax.broadcasted_iota(jnp.int32, (rows_c, rows_z), 1)
        return ones((r == (s // 16) * 4 + s % 4) & ((s % 16) // 4 == q))

    for chunk in (2, 0, 1):
        first = chunk == 2
        if chunk == 2:
            wait(2, rcv_c, 0, NT, sem_dr.at[2])
            rem = rcv_c[...].reshape(rows_c, NT)
            for q, (n, size) in enumerate(tiles):
                zc[:, n : n + size] = dot(unstack(q), rem[:, :size]).astype(jnp.bfloat16)
            rows = rows_z
            load = lambda: zc[...]
        else:
            wait(chunk, rcv.at[chunk], 0, width, sem_dr.at[chunk])
            rows = blocks * 16
            load = lambda chunk=chunk: rcv[chunk].reshape(blocks * 16, width)

        def step(s):
            if first:
                for copy in gu_copies(s):
                    copy.wait()
            r = dot(load(), gu[s])
            a, b = r[:, :FT], r[:, FT:]
            h[0:rows, pl.ds(pl.multiple_of(s * FT, FT), FT)] = (
                a * jax.nn.sigmoid(a) * b
            ).astype(jnp.bfloat16)

        def body(i, c):
            for u in range(UNROLL):
                step(i * UNROLL + u)
            return c

        lax.fori_loop(0, steps // UNROLL, body, 0)
        for s in range(steps // UNROLL * UNROLL, steps):
            step(s)

        if chunk == 2:
            wait(2, snd_c, 0, NT, sem_ds.at[2])
        else:
            wait(chunk, snd.at[chunk], 0, width, sem_ds.at[chunk])
        for t, (n, size) in enumerate(tiles):
            if first:
                dn_copy(t).wait()
            out = dot(h[0:rows], dn[:, n : n + size]).astype(jnp.bfloat16)
            if chunk == 2:
                zc[:, n : n + size] = out
                continue
            snd[chunk, :, :, n : n + size] = out.reshape(blocks, 16, size)
            if chunk == 0:
                ret[0, core, :, n : n + size] = snd[0, core, :, n : n + size]
            send(chunk, snd.at[chunk], ret.at[chunk], n, size, sem_cs.at[chunk], sem_cr.at[chunk, t], behind)
        if chunk == 2:
            for n in range(0, NT, FT):
                total = None
                for q in range(4):
                    if q * NT + n < width:
                        part = dot(stack(q), zc[:, q * NT + n : q * NT + n + FT])
                        total = part if total is None else total + part
                snd_c[:, :, n : n + FT] = total.astype(jnp.bfloat16).reshape(2 * blocks, 16, FT)
            ret_c[core] = snd_c[core]
            send(2, snd_c, ret_c, 0, NT, sem_cs.at[2], sem_cr.at[2, 0], behind)

    def weights(chunk, rows):
        row = lax.broadcasted_iota(jnp.int32, (tokens, rows), 1)
        code, quarter = row_code(row, chunk)
        w = jnp.where(code == down0, gates[:, 0:1], 0.0) + jnp.where(code == down1, gates[:, 1:2], 0.0)
        if chunk == 2:
            w = jnp.where(row % 4 < rest, w, 0.0)
        return w, quarter

    w0 = weights(0, blocks * 16)[0].astype(jnp.bfloat16)
    w1 = weights(1, blocks * 16)[0].astype(jnp.bfloat16)
    w2, quarter = weights(2, rows_c)
    wait(2, ret_c, 0, NT, sem_cr.at[2, 0])
    for t, (n, size) in enumerate(tiles):
        wait(0, ret.at[0], n, size, sem_cr.at[0, t])
        total = dot(
            jnp.where(quarter == t, w2, 0.0).astype(jnp.bfloat16),
            ret_c[:, :, :size].reshape(rows_c, size),
        )
        total += dot(w0, ret[0, :, :, n : n + size].reshape(blocks * 16, size))
        wait(1, ret.at[1], n, size, sem_cr.at[1, t])
        total += dot(w1, ret[1, :, :, n : n + size].reshape(blocks * 16, size))
        xs[:, n : n + size] = total.astype(jnp.bfloat16)
        pltpu.make_async_copy(
            xs.at[:, pl.ds(n, size)], y_hbm.at[0, 0, :, pl.ds(n, size)], sem_y.at[t]
        ).start()
    for chunk in range(2):
        wait(chunk, snd.at[chunk], 0, width, sem_cs.at[chunk])
    wait(2, snd_c, 0, NT, sem_cs.at[2])
    for t, (n, size) in enumerate(tiles):
        pltpu.make_async_copy(
            xs.at[:, pl.ds(n, size)], y_hbm.at[0, 0, :, pl.ds(n, size)], sem_y.at[t]
        ).wait()


def layer(side, slots, x, expert, slot, gate, wg, wu, wd):
    tokens, width = x.shape[2:]
    hidden = wg.shape[2]
    blocks = side * side
    tiles = -(-width // NT)
    vmem, hbm = pl.BlockSpec(memory_space=pltpu.VMEM), pl.BlockSpec(memory_space=pl.ANY)
    bf16, sem = jnp.bfloat16, pltpu.SemaphoreType.DMA
    return pl.pallas_call(
        functools.partial(kernel, side, slots),
        out_shape=jax.ShapeDtypeStruct(x.shape, bf16),
        in_specs=[hbm, vmem, vmem, vmem, hbm, hbm, hbm],
        out_specs=hbm,
        scratch_shapes=[
            pltpu.VMEM((tokens, width), bf16),
            pltpu.VMEM((hidden // FT, width, 2 * FT), bf16),
            pltpu.VMEM((hidden, width), bf16),
            pltpu.VMEM((blocks * 16, hidden), bf16),
            pltpu.VMEM((2 * blocks * 4, width), bf16),
            pltpu.VMEM((2, blocks, 16, width), bf16),
            pltpu.VMEM((2 * blocks, 16, NT), bf16),
            pltpu.VMEM((2, blocks, 16, width), bf16),
            pltpu.VMEM((2 * blocks, 16, NT), bf16),
            pltpu.VMEM((2, blocks, 16, width), bf16),
            pltpu.VMEM((2 * blocks, 16, NT), bf16),
            sem(()),
            sem((hidden // FT, 2)),
            sem((tiles,)),
            sem((3,)),
            sem((3,)),
            sem((3,)),
            sem((3, tiles)),
            sem((tiles,)),
        ],
        compiler_params=pltpu.CompilerParams(
            collective_id=0, has_side_effects=True, vmem_limit_bytes=67043328
        ),
        name="moe_layer",
    )(x, expert, slot, gate, wg, wu, wd)


def solution(mesh):
    members = mesh.shape["ep"]
    side = round(members**0.5)

    def step(x, expert, slot, gate, w_gate, w_up, w_down):
        experts, (tokens, top) = w_gate.shape[0], expert.shape[2:]
        slots = 5 * tokens * top // (4 * experts)
        act, w = P("dp", "ep"), P("ep")
        return jax.shard_map(
            functools.partial(layer, side, slots),
            mesh=mesh,
            in_specs=(act, act, act, act, w, w, w),
            out_specs=act,
            check_vma=False,
        )(x, expert, slot, gate, w_gate, w_up, w_down)

    return step
```

time: 181 us -> 93.1 us (0.51)
  the two profiles are of different devices: /device:TPU:96 before, /device:TPU:97 now
where the time goes in v1:
time: 93.1 us; the launch traced here: 92.9 us
  Pallas kernels  86.3 us (93%)
  local copies, waits for them, and re-layouts  6.58 us (7%)
    pallas_call x1, Pallas kernels, layer(): pl.pallas_call(functools.partial(kernel, side, slots), out_shape=jax.Shap...  86.3 us
    unnamed x4, local copies, waits for them, and re-layouts  6.58 us

profile of v1, /device:TPU:97, one launch (start us, length us, event | category | flops | bytes accessed | tf_op | source)
XLA Modules:
  0.0 92.9 jit_solution(12489035727448433333)
XLA Ops:
  0.0 1.5 %copy.8.expert_ref = s32[1,1,256,2]{3,2,1,0:T(8,128)} copy(s32[1,1,256,2]{2,3,1,0:T(2,128)} %param.8) | data formatting | bytes 4096 | tf_op args[1]
  1.5 1.5 %copy.9.slot_ref = s32[1,1,256,2]{3,2,1,0:T(8,128)} copy(s32[1,1,256,2]{2,3,1,0:T(2,128)} %param.9) | data formatting | bytes 4096 | tf_op args[2]
  3.0 1.5 %copy.10.gate_ref = f32[1,1,256,2]{3,2,1,0:T(8,128)} copy(f32[1,1,256,2]{2,3,1,0:T(2,128)} %param.10) | data formatting | bytes 4096 | tf_op args[3]
  4.4 86.3 %moe_layer.1 = bf16[1,1,256,1792]{3,2,1,0:T(8,128)(2,1)} custom-call(bf16[1,1,256,1792]{3,2,1,0:T(8,128)(2,1)} %x_hbm.1, s32[1,1,256,2]{3,2,1,0:T(8,128)} %copy.8.expert_ref, s32[1,1,256,2]{3,2,1,0:T(8,128)} %copy.9.slot_ref, f32[1,1,256,2]{3,2,1,0:T(8,128)} %copy.10.gate_ref, bf16[2,1792,4864]{2,1,0:T(8,128)(2,1)} %wg.1, bf16[2,1792,4864]{2,1,0:T(8,128)(2,1)} %wu.1, ...), custom_call_target="tpu_custom_call" | custom-call | tf_op jit(solution)/shard_map/moe_layer/pallas_call | solution.py:277
  90.7 2.2 %copy.12 = bf16[1,1,256,1792]{3,2,1,0:T(8,128)(2,1)} copy(bf16[1,1,256,1792]{3,2,1,0:T(8,128)(2,1)} %moe_layer.1) | data formatting | bytes 1835008

commit v2 on v1

v2 whole, which is shorter than its diff:
```python
import functools

import jax
import jax.numpy as jnp
from jax import lax
from jax.experimental import pallas as pl
from jax.experimental.pallas import tpu as pltpu
from jax.sharding import PartitionSpec as P

MESH = pl.DeviceIdType.MESH
FT = 256
NT = 512
ROWS = 16
UNROLL = 3
PARTS = (
    ((0, 0), (2, 0), (0, 2), (2, 2)),
    ((1, 1), (3, 3), (1, 3), (3, 1)),
    ((2, 1), (0, 3), (2, 3), (0, 1)),
    ((1, 2), (3, 0), (3, 2), (1, 0)),
)
CHUNKS = ((), (0,), (1, 2), (3,))


def dot(a, b):
    return jnp.dot(a, b, preferred_element_type=jnp.float32)


def kernel(
    side, slots,
    x_hbm, expert_ref, slot_ref, gate_ref, wg, wu, wd, y_hbm,
    xs, wts, gu, dn, h, zc, snd, snd_c, rcv, rcv_c, ret, ret_c,
    sem_x, sem_g, sem_d, sem_ds, sem_dr, sem_cs, sem_cr, sem_y,
):
    members = side * side
    tokens, width = xs.shape
    hidden = h.shape[1]
    steps = hidden // FT
    rest = slots - ROWS
    dp, ep = lax.axis_index("dp"), lax.axis_index("ep")
    core = lax.rem(dp, 2)
    base = dp - core
    px, py = ep // side, lax.rem(ep, side)
    tiles = [(n, min(NT, width - n)) for n in range(0, width, NT)]
    blocks = 2 * members
    size_p = blocks // len(PARTS)

    def place(i):
        q, b = i // size_p, (i % size_p) // 2
        return 2 * (b // 2) + q % 2, 2 * (b % 2) + (q + q // 2) % 2

    def ahead(i):
        dx, dy = place(i)
        return ((px + dx) % side) * side + (py + dy) % side

    def behind(i):
        dx, dy = place(i)
        return ((px + side - dx) % side) * side + (py + side - dy) % side

    def remote(parts):
        parts = parts or range(len(PARTS))
        return len(parts) * size_p - (0 in parts)

    def sends(parts):
        for q in parts or range(len(PARTS)):
            for dx, dy in PARTS[q]:
                i = q * size_p + 2 * (dx // 2 * 2 + dy // 2)
                if dx == dy == 0:
                    yield 1 - core
                else:
                    yield i
                    yield i + 1

    copy_x = pltpu.make_async_copy(x_hbm.at[0, 0], xs, sem_x)
    copy_x.start()

    barrier = pltpu.get_barrier_semaphore()

    def greet(i, c):
        j = (i + 1) // 2 * 2 + (i + 1 + core) % 2
        pl.semaphore_signal(
            barrier, inc=1, device_id=(base + j % 2, ahead(j)), device_id_type=MESH
        )
        return c

    lax.fori_loop(0, blocks - 1, greet, 0)

    def gu_copies(s):
        cols = pl.ds(pl.multiple_of(s * FT, FT), FT)
        return (
            pltpu.make_async_copy(wg.at[core, :, cols], gu.at[s, :, pl.ds(0, FT)], sem_g.at[s, 0]),
            pltpu.make_async_copy(wu.at[core, :, cols], gu.at[s, :, pl.ds(FT, FT)], sem_g.at[s, 1]),
        )

    def dn_copy(t):
        n, size = tiles[t]
        return pltpu.make_async_copy(wd.at[core, :, pl.ds(n, size)], dn.at[:, pl.ds(n, size)], sem_d.at[t])

    copy_x.wait()

    def start_gu(s, c):
        for copy in gu_copies(s):
            copy.start()
        return c

    lax.fori_loop(0, steps, start_gu, 0)
    for t in range(len(tiles)):
        dn_copy(t).start()

    slot, expert = slot_ref[0, 0], expert_ref[0, 0]
    code = jnp.where(slot < slots, expert * slots + slot, -1)
    across0, across1 = code[0:1], code[1:2]

    def upright(v):
        return jnp.transpose(jnp.broadcast_to(v, (128, tokens)))[:, 0:1]

    def row_code(row):
        i = row // 16
        return (2 * ahead(i) + i % 2) * slots + row % 16

    def rest_code(row):
        i, j = row // 16, row % 16
        code = (2 * ahead(i) + i % 2) * slots + ROWS + j % 4
        return jnp.where(j % 4 < rest, code, -2), j // 4

    def ones(mask):
        return jnp.where(mask, 1.0, 0.0).astype(jnp.bfloat16)

    def send(parts, src, dst, n, size, s_sem, r_sem, target):
        for j in sends(parts):
            there = core if isinstance(j, jax.Array) else j // 2 * 2 + core
            cols = pl.ds(n, size)
            pltpu.make_async_remote_copy(
                src_ref=src.at[j, :, cols],
                dst_ref=dst.at[there, :, cols],
                send_sem=s_sem,
                recv_sem=r_sem,
                device_id=(base + j % 2, target(j)),
                device_id_type=MESH,
            ).start()

    def wait(parts, ref, n, size, sem):
        part = ref.at[pl.ds(0, remote(parts)), :, pl.ds(n, size)]
        pltpu.make_async_copy(part, part, sem).wait()

    rows_c = blocks * 16
    rows_p = size_p * 16
    code, quarter = rest_code(lax.broadcasted_iota(jnp.int32, (rows_c, tokens), 0))
    hit = (code == across0) | (code == across1)
    picks = [ones(hit & (quarter == q)) for q in range(4)]
    for n in range(0, NT, FT):
        total = None
        for q in range(4):
            if q * NT + n < width:
                part = dot(picks[q], xs[:, q * NT + n : q * NT + n + FT])
                total = part if total is None else total + part
        snd_c[:, :, n : n + FT] = total.astype(jnp.bfloat16).reshape(blocks, 16, FT)
    rcv_c[core] = snd_c[core]

    pl.semaphore_wait(barrier, blocks - 1)
    send((), snd_c, rcv_c, 0, NT, sem_ds.at[0], sem_dr.at[0], ahead)
    for c, parts in enumerate(CHUNKS):
        for q in parts:
            i = q * size_p
            code = row_code(lax.broadcasted_iota(jnp.int32, (rows_p, tokens), 0) + q * rows_p)
            pick = ones((code == across0) | (code == across1))
            for n, size in tiles:
                z = dot(pick, xs[:, n : n + size]).astype(jnp.bfloat16)
                snd[i : i + size_p, :, n : n + size] = z.reshape(size_p, 16, size)
            if q == 0:
                rcv[core] = snd[core]
            send((q,), snd, rcv, 0, width, sem_ds.at[c], sem_dr.at[c], ahead)

    down0, down1 = upright(across0), upright(across1)
    gates = gate_ref[0, 0].astype(jnp.bfloat16).astype(jnp.float32)
    gate0, gate1 = upright(gates[0:1]), upright(gates[1:2])
    row = lax.broadcasted_iota(jnp.int32, (tokens, rows_c), 1)
    for i, code in enumerate((row_code(row), rest_code(row)[0])):
        w = jnp.where(code == down0, gate0, 0.0) + jnp.where(code == down1, gate1, 0.0)
        wts[:, i * rows_c : (i + 1) * rows_c] = w.astype(jnp.bfloat16)

    rows_z = zc.shape[0]

    def unstack(q):
        r = lax.broadcasted_iota(jnp.int32, (rows_z, rows_c), 0)
        s = lax.broadcasted_iota(jnp.int32, (rows_z, rows_c), 1)
        return ones(s == (r // 4) * 16 + q * 4 + r % 4)

    def stack(q):
        s = lax.broadcasted_iota(jnp.int32, (rows_c, rows_z), 0)
        r = lax.broadcasted_iota(jnp.int32, (rows_c, rows_z), 1)
        return ones((r == (s // 16) * 4 + s % 4) & ((s % 16) // 4 == q))

    for c, parts in enumerate(CHUNKS):
        first = c == 0
        if parts:
            wait(parts, rcv, 0, width, sem_dr.at[c])
            rows, i = len(parts) * rows_p, parts[0] * size_p
            load = lambda i=i, rows=rows: rcv[i : i + rows // 16].reshape(rows, width)
        else:
            wait((), rcv_c, 0, NT, sem_dr.at[c])
            rem = rcv_c[...].reshape(rows_c, NT)
            for q, (n, size) in enumerate(tiles):
                zc[:, n : n + size] = dot(unstack(q), rem[:, :size]).astype(jnp.bfloat16)
            rows = rows_z
            load = lambda: zc[...]

        def step(s):
            if first:
                for copy in gu_copies(s):
                    copy.wait()
            r = dot(load(), gu[s])
            a, b = r[:, :FT], r[:, FT:]
            h[0:rows, pl.ds(pl.multiple_of(s * FT, FT), FT)] = (
                a * jax.nn.sigmoid(a) * b
            ).astype(jnp.bfloat16)

        def body(i, c):
            for u in range(UNROLL):
                step(i * UNROLL + u)
            return c

        lax.fori_loop(0, steps // UNROLL, body, 0)
        for s in range(steps // UNROLL * UNROLL, steps):
            step(s)

        if parts:
            wait(parts, snd, 0, width, sem_ds.at[c])
        else:
            wait((), snd_c, 0, NT, sem_ds.at[c])
        for t, (n, size) in enumerate(tiles):
            if first:
                dn_copy(t).wait()
            out = dot(h[0:rows], dn[:, n : n + size]).astype(jnp.bfloat16)
            if not parts:
                zc[:, n : n + size] = out
                continue
            snd[i : i + rows // 16, :, n : n + size] = out.reshape(rows // 16, 16, size)
            if 0 in parts:
                ret[core, :, n : n + size] = snd[core, :, n : n + size]
            send(parts, snd, ret, n, size, sem_cs.at[c], sem_cr.at[c, t], behind)
        if not parts:
            for n in range(0, NT, FT):
                total = None
                for q in range(4):
                    if q * NT + n < width:
                        part = dot(stack(q), zc[:, q * NT + n : q * NT + n + FT])
                        total = part if total is None else total + part
                snd_c[:, :, n : n + FT] = total.astype(jnp.bfloat16).reshape(blocks, 16, FT)
            ret_c[core] = snd_c[core]
            send((), snd_c, ret_c, 0, NT, sem_cs.at[c], sem_cr.at[c, 0], behind)

    _, quarter = rest_code(lax.broadcasted_iota(jnp.int32, (tokens, rows_c), 1))
    early = rows_c - len(CHUNKS[-1]) * rows_p
    for t, (n, size) in enumerate(tiles):
        for c, parts in enumerate(CHUNKS[:-1]):
            if parts:
                wait(parts, ret, n, size, sem_cr.at[c, t])
            elif t == 0:
                wait((), ret_c, 0, NT, sem_cr.at[c, 0])
        w = wts[:, rows_c:].astype(jnp.float32)
        w = jnp.where(quarter == t, w, 0.0).astype(jnp.bfloat16)
        total = dot(w, ret_c[:, :, :size].reshape(rows_c, size))
        rows = ret[: early // 16, :, n : n + size].reshape(early, size)
        total += dot(wts[:, :early], rows)
        wait(CHUNKS[-1], ret, n, size, sem_cr.at[len(CHUNKS) - 1, t])
        rows = ret[early // 16 :, :, n : n + size].reshape(rows_c - early, size)
        total += dot(wts[:, early:rows_c], rows)
        xs[:, n : n + size] = total.astype(jnp.bfloat16)
        pltpu.make_async_copy(
            xs.at[:, pl.ds(n, size)], y_hbm.at[0, 0, :, pl.ds(n, size)], sem_y.at[t]
        ).start()
    for c, parts in enumerate(CHUNKS):
        if parts:
            wait(parts, snd, 0, width, sem_cs.at[c])
        else:
            wait((), snd_c, 0, NT, sem_cs.at[c])
    for t, (n, size) in enumerate(tiles):
        pltpu.make_async_copy(
            xs.at[:, pl.ds(n, size)], y_hbm.at[0, 0, :, pl.ds(n, size)], sem_y.at[t]
        ).wait()


def layer(side, slots, x, expert, slot, gate, wg, wu, wd):
    tokens, width = x.shape[2:]
    hidden = wg.shape[2]
    blocks = 2 * side * side
    tiles, chunks = -(-width // NT), len(CHUNKS)
    largest = max(map(len, CHUNKS)) * blocks // len(PARTS) * 16
    vmem, hbm = pl.BlockSpec(memory_space=pltpu.VMEM), pl.BlockSpec(memory_space=pl.ANY)
    bf16, sem = jnp.bfloat16, pltpu.SemaphoreType.DMA
    whole, quarters = pltpu.VMEM((blocks, 16, width), bf16), pltpu.VMEM((blocks, 16, NT), bf16)
    return pl.pallas_call(
        functools.partial(kernel, side, slots),
        out_shape=jax.ShapeDtypeStruct(x.shape, bf16),
        in_specs=[hbm, vmem, vmem, vmem, hbm, hbm, hbm],
        out_specs=hbm,
        scratch_shapes=[
            pltpu.VMEM((tokens, width), bf16),
            pltpu.VMEM((tokens, 2 * blocks * 16), bf16),
            pltpu.VMEM((hidden // FT, width, 2 * FT), bf16),
            pltpu.VMEM((hidden, width), bf16),
            pltpu.VMEM((largest, hidden), bf16),
            pltpu.VMEM((blocks * 4, width), bf16),
            whole,
            quarters,
            whole,
            quarters,
            whole,
            quarters,
            sem(()),
            sem((hidden // FT, 2)),
            sem((tiles,)),
            sem((chunks,)),
            sem((chunks,)),
            sem((chunks,)),
            sem((chunks, tiles)),
            sem((tiles,)),
        ],
        compiler_params=pltpu.CompilerParams(
            collective_id=0, has_side_effects=True, vmem_limit_bytes=67043328
        ),
        name="moe_layer",
    )(x, *(jnp.swapaxes(v, 2, 3) for v in (expert, slot, gate)), wg, wu, wd)


def solution(mesh):
    members = mesh.shape["ep"]
    side = round(members**0.5)

    def step(x, expert, slot, gate, w_gate, w_up, w_down):
        experts, (tokens, top) = w_gate.shape[0], expert.shape[2:]
        slots = 5 * tokens * top // (4 * experts)
        act, w = P("dp", "ep"), P("ep")
        return jax.shard_map(
            functools.partial(layer, side, slots),
            mesh=mesh,
            in_specs=(act, act, act, act, w, w, w),
            out_specs=act,
            check_vma=False,
        )(x, expert, slot, gate, w_gate, w_up, w_down)

    return step
```

time: 93.1 us -> 85.7 us (0.921)
  local copies, waits for them, and re-layouts: 6.58 us -> 2.16 us
  Pallas kernels: 86.3 us -> 83.3 us
    unnamed x4 -> x1, local copies, waits for them, and re-layouts: 6.58 us -> 2.16 us
    pallas_call x1, Pallas kernels: 86.3 us -> 83.3 us  [layer(): pl.pallas_call(functools.partial(kernel, side, slots), out_shape=jax.Shap...]
where the time goes in v2:
time: 85.7 us; the launch traced here: 85.5 us
  Pallas kernels  83.3 us (97%)
  local copies, waits for them, and re-layouts  2.16 us (3%)
    pallas_call x1, Pallas kernels, layer(): pl.pallas_call(functools.partial(kernel, side, slots), out_shape=jax.Shap...  83.3 us
    unnamed x1, local copies, waits for them, and re-layouts  2.16 us

profile of v2, /device:TPU:97, one launch (start us, length us, event | category | flops | bytes accessed | tf_op | source)
XLA Modules:
  0.0 85.5 jit_solution(10485060367273685491)
XLA Ops:
  0.0 83.3 %moe_layer.1 = bf16[1,1,256,1792]{3,2,1,0:T(8,128)(2,1)} custom-call(bf16[1,1,256,1792]{3,2,1,0:T(8,128)(2,1)} %x_hbm.1, s32[1,1,2,256]{3,2,1,0:T(2,128)} %bitcast.3, s32[1,1,2,256]{3,2,1,0:T(2,128)} %bitcast.4, f32[1,1,2,256]{3,2,1,0:T(2,128)} %bitcast.5, bf16[2,1792,4864]{2,1,0:T(8,128)(2,1)} %wg.1, bf16[2,1792,4864]{2,1,0:T(8,128)(2,1)} %wu.1, ...), custom_call_target="tpu_custom_call" | custom-call | tf_op jit(solution)/shard_map/moe_layer/pallas_call | solution.py:292
  83.3 2.2 %copy.9 = bf16[1,1,256,1792]{3,2,1,0:T(8,128)(2,1)} copy(bf16[1,1,256,1792]{3,2,1,0:T(8,128)(2,1)} %moe_layer.1) | data formatting | bytes 1835008

commit v3 on v1

--- a/solution.py
+++ b/solution.py
@@ -11,7 +11,11 @@
 FT = 256
 NT = 512
 ROWS = 16
-UNROLL = 3
+UNROLL = 6
+PHASES = (
+    ((0, 0), (2, 0), (0, 2), (1, 1), (3, 3), (1, 3), (3, 1), (2, 2)),
+    ((2, 1), (0, 3), (2, 3), (0, 1), (1, 2), (3, 0), (3, 2), (1, 0)),
+)
 
 
 def dot(a, b):
@@ -21,7 +25,7 @@
 def kernel(
     side, slots,
     x_hbm, expert_ref, slot_ref, gate_ref, wg, wu, wd, y_hbm,
-    xs, gu, dn, h, zc, snd, snd_c, rcv, rcv_c, ret, ret_c,
+    xs, wts, gu, dn, h, zc, snd, snd_c, rcv, rcv_c, ret, ret_c,
     sem_x, sem_g, sem_d, sem_ds, sem_dr, sem_cs, sem_cr, sem_y,
 ):
     members = side * side
@@ -37,8 +41,11 @@
     blocks = members
 
     def place(i, chunk):
-        dx = i // (2 * side)
-        return (dx if chunk == 2 else 2 * dx + chunk), (i // 2) % side
+        b = i // 2
+        if chunk == 2:
+            return b // side, b % side
+        dx = b // 2
+        return dx, 2 * (b % 2) + (dx + chunk) % 2
 
     def ahead(i, chunk):
         dx, dy = place(i, chunk)
@@ -51,11 +58,14 @@
     def others(chunk):
         return {0: blocks - 1, 1: blocks, 2: 2 * blocks - 1}[chunk]
 
-    def block_of(i, chunk):
-        if chunk == 1:
-            return i
-        i = i + 1
-        return i // 2 * 2 + (i + core) % 2
+    def sends(chunk):
+        for dx, dy in PHASES[0] + PHASES[1] if chunk == 2 else PHASES[chunk]:
+            b = dx * side + dy if chunk == 2 else 2 * dx + dy // 2
+            if dx == dy == 0:
+                yield 1 - core
+            else:
+                yield 2 * b
+                yield 2 * b + 1
 
     copy_x = pltpu.make_async_copy(x_hbm.at[0, 0], xs, sem_x)
     copy_x.start()
@@ -63,7 +73,7 @@
     barrier = pltpu.get_barrier_semaphore()
 
     def greet(i, c):
-        j = block_of(i, 2)
+        j = (i + 1) // 2 * 2 + (i + 1 + core) % 2
         pl.semaphore_signal(
             barrier, inc=1, device_id=(base + j % 2, ahead(j, 2)), device_id_type=MESH
         )
@@ -95,10 +105,10 @@
 
     slot, expert = slot_ref[0, 0], expert_ref[0, 0]
     code = jnp.where(slot < slots, expert * slots + slot, -1)
-    down0, down1 = code[:, 0:1], code[:, 1:2]
-    across0 = jnp.transpose(jnp.broadcast_to(down0, (tokens, 128)))[0:1]
-    across1 = jnp.transpose(jnp.broadcast_to(down1, (tokens, 128)))[0:1]
-    gates = gate_ref[0, 0].astype(jnp.bfloat16).astype(jnp.float32)
+    across0, across1 = code[0:1], code[1:2]
+
+    def upright(v):
+        return jnp.transpose(jnp.broadcast_to(v, (128, tokens)))[:, 0:1]
 
     def row_code(row, chunk):
         i, j = row // 16, row % 16
@@ -118,9 +128,8 @@
         return jnp.where(mask, 1.0, 0.0).astype(jnp.bfloat16)
 
     def send(chunk, src, dst, n, size, s_sem, r_sem, target):
-        def one(i, c):
-            j = block_of(i, chunk)
-            there = j // 2 * 2 + core
+        for j in sends(chunk):
+            there = core if isinstance(j, jax.Array) else j // 2 * 2 + core
             cols = pl.ds(n, size)
             pltpu.make_async_remote_copy(
                 src_ref=src.at[j, :, cols],
@@ -130,9 +139,6 @@
                 device_id=(base + j % 2, target(j, chunk)),
                 device_id_type=MESH,
             ).start()
-            return c
-
-        lax.fori_loop(0, others(chunk), one, 0)
 
     def wait(chunk, ref, n, size, sem):
         part = ref.at[pl.ds(0, others(chunk)), :, pl.ds(n, size)]
@@ -161,6 +167,19 @@
         if chunk == 0:
             rcv[0, core] = snd[0, core]
         send(chunk, snd.at[chunk], rcv.at[chunk], 0, width, sem_ds.at[chunk], sem_dr.at[chunk], ahead)
+
+    down0, down1 = upright(across0), upright(across1)
+    gates = gate_ref[0, 0].astype(jnp.bfloat16).astype(jnp.float32)
+    gate0, gate1 = upright(gates[0:1]), upright(gates[1:2])
+    at = 0
+    for chunk, rows in ((0, blocks * 16), (1, blocks * 16), (2, rows_c)):
+        row = lax.broadcasted_iota(jnp.int32, (tokens, rows), 1)
+        code, _ = row_code(row, chunk)
+        w = jnp.where(code == down0, gate0, 0.0) + jnp.where(code == down1, gate1, 0.0)
+        if chunk == 2:
+            w = jnp.where(row % 4 < rest, w, 0.0)
+        wts[:, at : at + rows] = w.astype(jnp.bfloat16)
+        at += rows
 
     rows_z = zc.shape[0]
 
@@ -233,17 +252,10 @@
             ret_c[core] = snd_c[core]
             send(2, snd_c, ret_c, 0, NT, sem_cs.at[2], sem_cr.at[2, 0], behind)
 
-    def weights(chunk, rows):
-        row = lax.broadcasted_iota(jnp.int32, (tokens, rows), 1)
-        code, quarter = row_code(row, chunk)
-        w = jnp.where(code == down0, gates[:, 0:1], 0.0) + jnp.where(code == down1, gates[:, 1:2], 0.0)
-        if chunk == 2:
-            w = jnp.where(row % 4 < rest, w, 0.0)
-        return w, quarter
-
-    w0 = weights(0, blocks * 16)[0].astype(jnp.bfloat16)
-    w1 = weights(1, blocks * 16)[0].astype(jnp.bfloat16)
-    w2, quarter = weights(2, rows_c)
+    w0 = wts[:, 0 : blocks * 16]
+    w1 = wts[:, blocks * 16 : 2 * blocks * 16]
+    w2 = wts[:, 2 * blocks * 16 :].astype(jnp.float32)
+    _, quarter = row_code(lax.broadcasted_iota(jnp.int32, (tokens, rows_c), 1), 2)
     wait(2, ret_c, 0, NT, sem_cr.at[2, 0])
     for t, (n, size) in enumerate(tiles):
         wait(0, ret.at[0], n, size, sem_cr.at[0, t])
@@ -281,6 +293,7 @@
         out_specs=hbm,
         scratch_shapes=[
             pltpu.VMEM((tokens, width), bf16),
+            pltpu.VMEM((tokens, 4 * blocks * 16), bf16),
             pltpu.VMEM((hidden // FT, width, 2 * FT), bf16),
             pltpu.VMEM((hidden, width), bf16),
             pltpu.VMEM((blocks * 16, hidden), bf16),
@@ -304,7 +317,7 @@
             collective_id=0, has_side_effects=True, vmem_limit_bytes=67043328
         ),
         name="moe_layer",
-    )(x, expert, slot, gate, wg, wu, wd)
+    )(x, *(jnp.swapaxes(v, 2, 3) for v in (expert, slot, gate)), wg, wu, wd)
 
 
 def solution(mesh):

time: 93.1 us -> 79.4 us (0.85)
  Pallas kernels: 86.3 us -> 77 us
  local copies, waits for them, and re-layouts: 6.58 us -> 2.16 us
    pallas_call x1, Pallas kernels: 86.3 us -> 77 us  [layer(): pl.pallas_call(functools.partial(kernel, side, slots), out_shape=jax.Shap...]
    unnamed x4 -> x1, local copies, waits for them, and re-layouts: 6.58 us -> 2.16 us
where the time goes in v3:
time: 79.4 us; the launch traced here: 79.2 us
  Pallas kernels  77 us (97%)
  local copies, waits for them, and re-layouts  2.16 us (3%)
    pallas_call x1, Pallas kernels, layer(): pl.pallas_call(functools.partial(kernel, side, slots), out_shape=jax.Shap...  77 us
    unnamed x1, local copies, waits for them, and re-layouts  2.16 us

profile of v3, /device:TPU:97, one launch (start us, length us, event | category | flops | bytes accessed | tf_op | source)
XLA Modules:
  0.0 79.2 jit_solution(13838517727393923031)
XLA Ops:
  0.0 77.0 %moe_layer.1 = bf16[1,1,256,1792]{3,2,1,0:T(8,128)(2,1)} custom-call(bf16[1,1,256,1792]{3,2,1,0:T(8,128)(2,1)} %x_hbm.1, s32[1,1,2,256]{3,2,1,0:T(2,128)} %bitcast.3, s32[1,1,2,256]{3,2,1,0:T(2,128)} %bitcast.4, f32[1,1,2,256]{3,2,1,0:T(2,128)} %bitcast.5, bf16[2,1792,4864]{2,1,0:T(8,128)(2,1)} %wg.1, bf16[2,1792,4864]{2,1,0:T(8,128)(2,1)} %wu.1, ...), custom_call_target="tpu_custom_call" | custom-call | tf_op jit(solution)/shard_map/moe_layer/pallas_call | solution.py:289
  77.0 2.2 %copy.9 = bf16[1,1,256,1792]{3,2,1,0:T(8,128)(2,1)} copy(bf16[1,1,256,1792]{3,2,1,0:T(8,128)(2,1)} %moe_layer.1) | data formatting | bytes 1835008
